TPU v7x, 32 devices: a whole 2x2x4 slice. The times are simulated.
32 devices in a mesh: row: 4 (over y, core), col: 8 (over z, x).
Axes of the slice: x: 2, y: 2, z: 4, core: 2. Of those that a mesh axis runs over, the one named last changes fastest.
Arguments:
- density: float32 [4096, 32768], P('row', 'col'), may hold values from 0 to 1
- design_mask: int32 [32, 256], P('row', 'col'), may hold values 0 or 1
- rebalance: int32 [8192], replicated, may hold values from 0 to 8191, as said below
Outputs:
- balanced: bfloat16 [8192, 128, 128], P(('row', 'col'))
- constraint: float32 [], replicated
Inputs may be any that keep to these rules, and one draw needn't show every extreme that they name: `rebalance`: A permutation of the 8192 block numbers. Of the blocks that one device holds, the ones that land among one device's output blocks number exactly 8 or none.
All inputs are finite; a program needn't handle non-finite values. No bound on the sum of `design_mask` on one device may be relied on, other than what follows from the above.
Results may differ from a plain program's by a relative error of at most 0.001.
Values may be sent and summed in bfloat16 or wider, within the bound.
A program may use at most 192 MiB of HBM per device.

v0:
```python
import functools

import jax
import jax.numpy as jnp
import numpy as np
from jax import lax
from jax.experimental import pallas as pl
from jax.experimental.pallas import tpu as pltpu
from jax.sharding import PartitionSpec as P

BS = 128
RADIUS = 16
SHARPNESS = 32.0
THRESHOLD = 0.5
VOLUME_TARGET = 0.4
MESH = pl.DeviceIdType.MESH
MIB = 2**20
GROUP = 4
STRIP = BS // RADIUS
SIDES = [(dr, dc) for dr in (-1, 0, 1) for dc in (-1, 0, 1) if dr or dc]


def filter_taps():
    sigma = RADIUS / 4.0
    offsets = np.arange(2 * RADIUS + 1, dtype=np.float64) - RADIUS
    raw_taps = np.exp(-offsets * offsets / (2.0 * sigma * sigma))
    return (raw_taps / raw_taps.sum()).astype(np.float32)


def split(x):
    high = x.astype(jnp.bfloat16)
    return high, (x - high.astype(jnp.float32)).astype(jnp.bfloat16)


def bands():
    taps = filter_taps()
    rows = np.zeros((BS, BS + 2 * RADIUS), np.float32)
    cols = np.zeros((2 * BS, BS), np.float32)
    for out in range(BS):
        for e in range(2 * RADIUS + 1):
            rows[out, out + e] = taps[e]
            source = out + e - RADIUS
            at = source if 0 <= source < BS else BS + source % BS
            cols[at, out] = taps[e]
    return split(jnp.asarray(rows)) + split(jnp.asarray(cols))


def over(x, n):
    if n & (n - 1) == 0:
        return x >> (n.bit_length() - 1), x & (n - 1)
    return lax.div(x, jnp.int32(n)), lax.rem(x, jnp.int32(n))


def project_block(before, own, after, mask, row_high, row_low, col_high, col_low):
    lane = lax.broadcasted_iota(jnp.int32, own.shape, 1)
    side = jnp.where(lane < BS // 2, after, before)
    high, low = split(jnp.concatenate([own, side], axis=1))
    dot = functools.partial(jnp.dot, preferred_element_type=jnp.float32)
    along = dot(high, col_high[...]) + (dot(low, col_high[...]) + dot(high, col_low[...]))
    high, low = split(along)
    filtered = dot(row_high[...], high) + (dot(row_high[...], low) + dot(row_low[...], high))
    lower = float(np.tanh(np.float32(SHARPNESS * THRESHOLD)))
    upper = float(np.tanh(np.float32(SHARPNESS * (1.0 - THRESHOLD))))
    return (lower + jnp.tanh(SHARPNESS * (filtered - THRESHOLD))) * (mask.astype(jnp.float32) / (lower + upper))


def upto_lane(x):
    lane = lax.broadcasted_iota(jnp.int32, x.shape, 1)
    step = 1
    while step < x.shape[1]:
        x = x + jnp.where(lane >= step, pltpu.roll(x, step, 1), 0)
        step *= 2
    return x


def locate(wanted, mask_rows, mask_cols, col_count):
    block_row, block_col = over(wanted, mask_cols * col_count)
    row_dev, row_in = over(block_row, mask_rows)
    col_dev, col_in = over(block_col, mask_cols)
    return row_dev * col_count + col_dev, row_in * mask_cols + col_in


def pick(chosen, rank, values, capacity):
    lane = lax.broadcasted_iota(jnp.int32, chosen.shape, 1)
    out = jnp.zeros(chosen.shape, jnp.int32)
    for k in range(capacity):
        found = jnp.sum(jnp.where(chosen & (rank == k + 1), values, 0), axis=1, keepdims=True)
        out = jnp.where(lane == k, found, out)
    return out


def send_order(wanted, me, per, mask_rows, mask_cols, col_count, capacity):
    source, local = locate(wanted, mask_rows, mask_cols, col_count)
    mine = source == me
    rank = upto_lane(mine.astype(jnp.int32))
    count = jnp.broadcast_to(rank[:, BS - 1 :], rank.shape)
    _, part = over(lax.broadcasted_iota(jnp.int32, rank.shape, 0), per)
    for j in range(1, per):
        rank = rank + jnp.where(part >= j, pltpu.roll(count, j, 0), 0)
    return pick(mine, rank, local, capacity)


def landing(wanted, devices, mask_rows, mask_cols, col_count, capacity):
    row = lax.broadcasted_iota(jnp.int32, (devices, BS), 0)
    lane = lax.broadcasted_iota(jnp.int32, (devices, BS), 1)
    before = jnp.zeros((devices, 1), jnp.int32)
    out = jnp.zeros((devices, BS), jnp.int32)
    for j in range(wanted.shape[0]):
        source, _ = locate(jnp.broadcast_to(wanted[j : j + 1], (devices, BS)), mask_rows, mask_cols, col_count)
        here = source == row
        rank = upto_lane(here.astype(jnp.int32)) + before
        before = rank[:, BS - 1 :]
        out = out + pick(here, rank, lane + j * BS, capacity)
    return out


def exchange_kernel(
    sizes, mask, density, rebalance, rh_in, rl_in, ch_in, cl_in,
    arrived, volume, slots, padded, outgoing, total, sums, wanted, order, table, rh, rl, ch, cl,
    strip_out, strip_in, rows_in, load_sem, small_sem, side_send, side_recv, send_sem, recv_sem, sum_send, sum_recv,
):
    row_count, col_count = sizes
    devices, capacity = outgoing.shape[:2]
    group = min(GROUP, capacity)
    mask_rows, mask_cols = mask.shape
    bands_of_rows, _, width = density.shape
    height = bands_of_rows * RADIUS
    last = bands_of_rows + 1
    per = wanted.shape[0] // devices
    row, col = lax.axis_index("row"), lax.axis_index("col")
    me = row * col_count + col
    half, quarter = col_count // 2, col_count // 4
    near = quarter * row_count

    def place_of(device):
        return (device // col_count, device % col_count)

    def target(turn):
        early = 1 - turn // (3 * near)
        is_beside = early * (turn % 3 // 2)
        is_across = early - is_beside
        across, beside, close = turn // 3 * 2 + turn % 3, turn // 3, (turn + 1) % near
        far_col = ((col // half + 1) % 2) * half + (col + across) % half
        beside_col = col // half * half + ((col // quarter + 1) % 2) * quarter + (col + beside) % quarter
        close_col = col // quarter * quarter + (col + close) % quarter
        to_col = is_across * far_col + is_beside * beside_col + (1 - early) * close_col
        step = is_across * (across // half) + is_beside * (beside // quarter) + (1 - early) * (close // quarter)
        return (row + step) % row_count * col_count + to_col

    def send(device, k):
        part = pl.ds(k, group)
        return pltpu.make_async_remote_copy(
            src_ref=outgoing.at[device, part], dst_ref=arrived.at[me, part], send_sem=send_sem.at[device],
            recv_sem=recv_sem.at[me], device_id=place_of(device), device_id_type=MESH,
        )

    def receive(device):
        return pltpu.make_async_remote_copy(
            src_ref=outgoing.at[device], dst_ref=arrived.at[device], send_sem=send_sem.at[device],
            recv_sem=recv_sem.at[device], device_id=place_of(device), device_id_type=MESH,
        )

    def send_sum(device):
        return pltpu.make_async_remote_copy(
            src_ref=sums.at[me], dst_ref=sums.at[me], send_sem=sum_send.at[device],
            recv_sem=sum_recv.at[me], device_id=place_of(device), device_id_type=MESH,
        )

    def receive_sum(device):
        return pltpu.make_async_remote_copy(
            src_ref=sums.at[me], dst_ref=sums.at[device], send_sem=sum_send.at[device],
            recv_sem=sum_recv.at[device], device_id=place_of(device), device_id_type=MESH,
        )

    def side_copy(dr, dc):
        at = SIDES.index((dr, dc))
        band, goal_band = {-1: 0, 1: bands_of_rows - 1}, {-1: last, 1: 0}
        cols = {-1: pl.ds(0, BS), 1: pl.ds(width - BS, BS)}
        goal_col = {-1: mask_cols + 1, 1: 0}
        if dr == 0:
            source, goal = strip_out.at[(dc + 1) // 2], strip_in.at[(dc + 1) // 2]
        elif dc == 0:
            source, goal = density.at[band[dr]], rows_in.at[(dr + 1) // 2]
        else:
            source, goal = density.at[band[dr], :, cols[dc]], padded.at[goal_col[dc], goal_band[dr]]
        return pltpu.make_async_remote_copy(
            src_ref=source, dst_ref=goal, send_sem=side_send.at[at], recv_sem=side_recv.at[at],
            device_id=(row + dr, col + dc), device_id_type=MESH,
        )

    def there(dr, dc):
        return (row + dr >= 0) & (row + dr < row_count) & (col + dc >= 0) & (col + dc < col_count)

    barrier = pltpu.get_barrier_semaphore()

    @pl.loop(1, devices)
    def _(o):
        pl.semaphore_signal(barrier, inc=1, device_id=place_of((me + o) % devices), device_id_type=MESH)

    small = [
        pltpu.make_async_copy(source, goal, small_sem.at[i])
        for i, (source, goal) in enumerate(
            [(rebalance, wanted), (rh_in, rh), (rl_in, rl), (ch_in, ch), (cl_in, cl)]
        )
    ]

    def load(c, sem):
        source = density.at[:, :, pl.ds(pl.multiple_of(c * BS, BS), BS)]
        return pltpu.make_async_copy(source, padded.at[c + 1, pl.ds(1, bands_of_rows)], load_sem.at[sem])

    edges = [load(0, 0), load(mask_cols - 1, 1)]
    small[0].start()
    for copy in edges + small[1:]:
        copy.start()

    @pl.loop(1, mask_cols - 1)
    def _(c):
        load(c, 2).start()

    total[...] = jnp.zeros_like(total)

    @pl.when(row == 0)
    def _():
        padded[:, 0] = jnp.zeros((mask_cols + 2, RADIUS, BS), jnp.float32)

    @pl.when(row == row_count - 1)
    def _():
        padded[:, last] = jnp.zeros((mask_cols + 2, RADIUS, BS), jnp.float32)

    @pl.when(col == 0)
    def _():
        padded[0] = jnp.zeros(padded.shape[1:], jnp.float32)

    @pl.when(col == col_count - 1)
    def _():
        padded[mask_cols + 1] = jnp.zeros(padded.shape[1:], jnp.float32)

    piece = height // STRIP
    parts = piece // RADIUS
    spot, _ = over(lax.broadcasted_iota(jnp.int32, (piece, BS), 1), RADIUS)
    for side, copy in enumerate(edges):
        copy.wait()
        strip = jnp.zeros((piece, BS), jnp.float32)
        for p in range(STRIP):
            edge = padded[1 + side * (mask_cols - 1), pl.ds(1 + p * parts, parts)].reshape(piece, BS)
            strip = jnp.where(spot == p, pltpu.roll(edge, (p * RADIUS + side * RADIUS) % BS, 1), strip)
        strip_out[side] = strip

    small[0].wait()
    order[...] = send_order(wanted[...], me, per, mask_rows, mask_cols, col_count, capacity)
    pl.semaphore_wait(barrier, devices - 1)
    for dr, dc in SIDES:

        @pl.when(there(dr, dc))
        def _():
            side_copy(dr, dc).start()

    to_scalars = pltpu.make_async_copy(order, table, small_sem.at[5])
    to_scalars.start()
    slots[...] = landing(
        wanted[pl.ds(me * per, per), :], devices, mask_rows, mask_cols, col_count, capacity
    )
    for dr, dc in SIDES:

        @pl.when(there(-dr, -dc))
        def _():
            side_copy(dr, dc).wait_recv()
            if dr == 0:
                strip = strip_in[(dc + 1) // 2]
                for p in range(STRIP):
                    shift = (BS - p * RADIUS - (dc + 1) // 2 * RADIUS) % BS
                    moved = pltpu.roll(strip, shift, 1).reshape(parts, RADIUS, BS)
                    padded[0 if dc == 1 else mask_cols + 1, pl.ds(1 + p * parts, parts)] = moved
            elif dc == 0:
                for c in range(mask_cols):
                    padded[c + 1, 0 if dr == 1 else last] = rows_in[(dr + 1) // 2, :, pl.ds(c * BS, BS)]

        @pl.when(there(dr, dc))
        def _():
            side_copy(dr, dc).wait_send()

    middle = padded.at[pl.ds(2, mask_cols - 2), pl.ds(1, bands_of_rows)]
    pltpu.make_async_copy(middle, middle, load_sem.at[2]).wait()
    for copy in small[1:]:
        copy.wait()
    to_scalars.wait()

    @pl.loop(0, devices * capacity)
    def _(n):
        turn, k = n // capacity, n % capacity
        device = target(turn)
        local = table[device * per, k]
        for j in range(1, per):
            local = local + table[device * per + j, k]
        r, c = over(local, mask_cols)
        deep = BS // RADIUS
        before, own, after = (
            jnp.concatenate([padded[c + i, r * deep + j] for j in range(deep + 2)], axis=0) for i in range(3)
        )
        cells = project_block(before, own, after, mask[r, c], rh, rl, ch, cl)
        total[...] += cells
        outgoing[device, k] = cells.astype(jnp.bfloat16)

        @pl.when((n % group == 0) & (n > 0) & (n <= (devices - 1) * capacity))
        def _():
            send(target((n - 1) // capacity), (n - 1) % capacity // group * group).start()

    sums[me] = jnp.sum(total[...].reshape(BS // 8, 8, BS), axis=0)
    arrived[me] = outgoing[me]

    @pl.loop(1, devices)
    def _(o):
        send_sum((me + o) % devices).start()

    @pl.loop(1, devices)
    def _(o):
        other = (me + o) % devices
        send_sum(other).wait_send()
        receive_sum(other).wait_recv()

    volume[...] = jnp.sum(sums[...], axis=0)

    @pl.loop(1, devices)
    def _(o):
        other = (me + o) % devices
        receive(other).wait_send()
        receive(other).wait_recv()


def exchange(mask, density, rebalance, sizes):
    devices = sizes[0] * sizes[1]
    capacity = mask.size // devices
    height, width = density.shape
    in_hbm = pl.BlockSpec(memory_space=pltpu.HBM)
    whole = pl.BlockSpec(memory_space=pltpu.VMEM)
    scalar = pl.BlockSpec(memory_space=pltpu.SMEM)
    cells = devices * capacity * BS * BS
    band = bands()
    wanted = rebalance.reshape(-1, BS)
    table = pltpu.VMEM(wanted.shape, jnp.int32)
    strips = pltpu.VMEM((2, height // STRIP, BS), jnp.float32)
    return pl.pallas_call(
        functools.partial(exchange_kernel, sizes),
        out_shape=(
            jax.ShapeDtypeStruct((devices, capacity, BS, BS), jnp.bfloat16),
            jax.ShapeDtypeStruct((8, BS), jnp.float32),
            jax.ShapeDtypeStruct((devices, BS), jnp.int32),
        ),
        in_specs=[scalar] + [in_hbm] * 6,
        out_specs=(whole, whole, whole),
        scratch_shapes=[
            pltpu.VMEM((width // BS + 2, height // RADIUS + 2, RADIUS, BS), jnp.float32),
            pltpu.VMEM((devices, capacity, BS, BS), jnp.bfloat16),
            pltpu.VMEM((BS, BS), jnp.float32),
            pltpu.VMEM((devices, 8, BS), jnp.float32),
            table,
            table,
            pltpu.SMEM(wanted.shape, jnp.int32),
        ]
        + [pltpu.VMEM(x.shape, x.dtype) for x in band]
        + [
            strips,
            strips,
            pltpu.VMEM((2, RADIUS, width), jnp.float32),
            pltpu.SemaphoreType.DMA((3,)),
            pltpu.SemaphoreType.DMA((6,)),
            pltpu.SemaphoreType.DMA((len(SIDES),)),
            pltpu.SemaphoreType.DMA((len(SIDES),)),
        ]
        + [pltpu.SemaphoreType.DMA((devices,))] * 4,
        compiler_params=pltpu.CompilerParams(vmem_limit_bytes=40 * MIB, collective_id=0, has_side_effects=True),
        cost_estimate=pl.CostEstimate(flops=cells * 2000, bytes_accessed=density.size * 4, transcendentals=cells),
        name="exchange",
    )(mask, density.reshape(height // RADIUS, RADIUS, width), wanted, *band)


def place_kernel(cells, slots, arrived, volume, out, constraint, store_sem):
    devices, capacity = arrived.shape[:2]

    @pl.loop(0, devices)
    def _(d):
        for k in range(capacity):
            pltpu.make_async_copy(arrived.at[d, k], out.at[slots[d, k]], store_sem).start()

    mean = jnp.sum(volume[...], keepdims=True) / cells
    constraint[...] = mean / VOLUME_TARGET - 1.0
    landed = out.at[pl.ds(0, devices * capacity)]
    pltpu.make_async_copy(landed, landed, store_sem).wait()


def place(slots, arrived, volume, cells):
    count = arrived.shape[0] * arrived.shape[1]
    whole = pl.BlockSpec(memory_space=pltpu.VMEM)
    return pl.pallas_call(
        functools.partial(place_kernel, cells),
        out_shape=(
            jax.ShapeDtypeStruct((count, BS, BS), jnp.bfloat16),
            jax.ShapeDtypeStruct((1, 1), jnp.float32),
        ),
        in_specs=[pl.BlockSpec(memory_space=pltpu.SMEM), whole, whole],
        out_specs=(pl.BlockSpec(memory_space=pltpu.HBM), whole),
        scratch_shapes=[pltpu.SemaphoreType.DMA],
        compiler_params=pltpu.CompilerParams(vmem_limit_bytes=8 * MIB),
        cost_estimate=pl.CostEstimate(flops=0, bytes_accessed=2 * arrived.size * 2, transcendentals=0),
        name="place",
    )(slots, arrived, volume)


def per_device(density, design_mask, rebalance):
    sizes = (lax.axis_size("row"), lax.axis_size("col"))
    arrived, volume, slots = exchange(design_mask, density, rebalance, sizes)
    balanced, constraint = place(slots, arrived, volume, float(density.size * sizes[0] * sizes[1]))
    return balanced, constraint[0, 0]


def solution(mesh):
    return jax.shard_map(
        per_device,
        mesh=mesh,
        in_specs=(P("row", "col"), P("row", "col"), P()),
        out_specs=(P(("row", "col"), None, None), P()),
        check_vma=False,
    )
```

profile of v0, /device:TPU:0, one launch (start us, length us, event | category | flops | bytes accessed | tf_op | source)
XLA Modules:
  0.0 222.4 jit_solution(11522187524934436072)
XLA Ops:
  0.6 0.0 copy-start
  0.6 0.7 copy-done
  1.4 0.0 copy-start.1
  1.4 0.7 copy-done.1
  2.1 0.0 copy-start.2
  2.1 0.8 copy-done.2
  2.9 0.0 copy-start.3
  2.9 0.8 copy-done.3
  3.8 0.0 copy-start.4
  3.8 0.8 copy-done.4
  4.6 0.0 copy-start.5
  4.6 0.8 copy-done.5
  5.4 212.5 %exchange.1 = (bf16[32,8,128,128]{3,2,1,0:T(8,128)(2,1)S(1)}, f32[8,128]{1,0:T(8,128)S(1)}, s32[32,128]{1,0:T(8,128)S(1)}) custom-call(s32[8,32]{1,0:T(8,128)S(1)} %copy-done.1, f32[64,16,4096]{2,1,0:T(8,128)} %bitcast.4, s32[64,128]{1,0:T(8,128)S(1)} %bitcast.3, bf16[128,160]{1,0:T(8,128)(2,1)S(1)} %copy-done.5, bf16[128,160]{1,0:T(8,128)(2,1)S(1)} %copy-done.4, ...), custom_call_target="tpu_custom_call" | custom-call | flops 8388608000 | bytes 16777216 | tf_op jit(solution)/shard_map/exchange/pallas_call | solution.py:342
  217.9 4.5 %place.1 = (bf16[256,128,128]{2,1,0:T(8,128)(2,1)}, f32[1,1]{1,0:T(1,128)}) custom-call(s32[32,128]{1,0:T(8,128)S(1)} %get-tuple-element.7.slots, bf16[32,8,128,128]{3,2,1,0:T(8,128)(2,1)S(1)} %get-tuple-element.8.arrived, f32[8,128]{1,0:T(8,128)S(1)} %get-tuple-element.9.volume), custom_call_target="tpu_custom_call" | custom-call | bytes 16777216 | tf_op jit(solution)/shard_map/place/pallas_call | solution.py:394
Async XLA Ops:
  0.6 0.8 copy-start
  1.4 0.7 copy-start.1
  2.1 0.8 copy-start.2
  2.9 0.8 copy-start.3
  3.8 0.8 copy-start.4
  4.6 0.8 copy-start.5
where the time goes:
time: 224 us; the launch traced here: 222 us
  Pallas kernels  217 us (97%)
  local copies, waits for them, and re-layouts  4.79 us (2%)
    pallas_call x1, Pallas kernels, exchange(): pl.pallas_call(functools.partial(exchange_kernel, sizes), out_shape=(jax....  212 us
    unnamed x12, local copies, waits for them, and re-layouts  4.79 us
    pallas_call x1, Pallas kernels, place(): pl.pallas_call(functools.partial(place_kernel, cells), out_shape=(jax.Sha...  4.49 us

commit v1 on v0

--- a/solution.py
+++ b/solution.py
@@ -15,7 +15,7 @@
 VOLUME_TARGET = 0.4
 MESH = pl.DeviceIdType.MESH
 MIB = 2**20
-GROUP = 4
+GROUP = 2
 STRIP = BS // RADIUS
 SIDES = [(dr, dc) for dr in (-1, 0, 1) for dc in (-1, 0, 1) if dr or dc]
 
@@ -32,17 +32,23 @@
     return high, (x - high.astype(jnp.float32)).astype(jnp.bfloat16)
 
 
-def bands():
+def band(distance):
     taps = filter_taps()
-    rows = np.zeros((BS, BS + 2 * RADIUS), np.float32)
-    cols = np.zeros((2 * BS, BS), np.float32)
-    for out in range(BS):
-        for e in range(2 * RADIUS + 1):
-            rows[out, out + e] = taps[e]
-            source = out + e - RADIUS
-            at = source if 0 <= source < BS else BS + source % BS
-            cols[at, out] = taps[e]
-    return split(jnp.asarray(rows)) + split(jnp.asarray(cols))
+    weight = jnp.zeros(distance.shape, jnp.float32)
+    for far in range(RADIUS + 1):
+        weight = jnp.where(distance == far, float(taps[RADIUS + far]), weight)
+    return split(weight)
+
+
+def col_bands():
+    source = lax.broadcasted_iota(jnp.int32, (2 * BS, BS), 0)
+    source = jnp.where(source < BS + BS // 2, source, source - 2 * BS)
+    return band(jnp.abs(source - lax.broadcasted_iota(jnp.int32, source.shape, 1)))
+
+
+def row_bands():
+    source = lax.broadcasted_iota(jnp.int32, (BS, BS + 2 * RADIUS), 1) - RADIUS
+    return band(jnp.abs(source - lax.broadcasted_iota(jnp.int32, source.shape, 0)))
 
 
 def over(x, n):
@@ -115,14 +121,14 @@
 
 
 def exchange_kernel(
-    sizes, mask, density, rebalance, rh_in, rl_in, ch_in, cl_in,
-    arrived, volume, slots, padded, outgoing, total, sums, wanted, order, table, rh, rl, ch, cl,
-    strip_out, strip_in, rows_in, load_sem, small_sem, side_send, side_recv, send_sem, recv_sem, sum_send, sum_recv,
+    sizes, mask_rows, mask_cols, density, known,
+    arrived, volume, slots, padded, outgoing, total, sums, order, table, rh, rl, ch, cl,
+    strip_out, strip_in, rows_out, rows_in, load_sem, side_send, side_recv, send_sem, recv_sem, sum_send, sum_recv,
 ):
     row_count, col_count = sizes
     devices, capacity = outgoing.shape[:2]
     group = min(GROUP, capacity)
-    mask_rows, mask_cols = mask.shape
+    wanted = known[: known.shape[0] - mask_rows]
     bands_of_rows, _, width = density.shape
     height = bands_of_rows * RADIUS
     last = bands_of_rows + 1
@@ -174,15 +180,15 @@
 
     def side_copy(dr, dc):
         at = SIDES.index((dr, dc))
-        band, goal_band = {-1: 0, 1: bands_of_rows - 1}, {-1: last, 1: 0}
+        edge, goal_band = {-1: 0, 1: bands_of_rows - 1}, {-1: last, 1: 0}
         cols = {-1: pl.ds(0, BS), 1: pl.ds(width - BS, BS)}
         goal_col = {-1: mask_cols + 1, 1: 0}
         if dr == 0:
             source, goal = strip_out.at[(dc + 1) // 2], strip_in.at[(dc + 1) // 2]
         elif dc == 0:
-            source, goal = density.at[band[dr]], rows_in.at[(dr + 1) // 2]
+            source, goal = rows_out.at[(dr + 1) // 2], rows_in.at[(dr + 1) // 2]
         else:
-            source, goal = density.at[band[dr], :, cols[dc]], padded.at[goal_col[dc], goal_band[dr]]
+            source, goal = density.at[edge[dr], :, cols[dc]], padded.at[goal_col[dc], goal_band[dr]]
         return pltpu.make_async_remote_copy(
             src_ref=source, dst_ref=goal, send_sem=side_send.at[at], recv_sem=side_recv.at[at],
             device_id=(row + dr, col + dc), device_id_type=MESH,
@@ -197,20 +203,16 @@
     def _(o):
         pl.semaphore_signal(barrier, inc=1, device_id=place_of((me + o) % devices), device_id_type=MESH)
 
-    small = [
-        pltpu.make_async_copy(source, goal, small_sem.at[i])
-        for i, (source, goal) in enumerate(
-            [(rebalance, wanted), (rh_in, rh), (rl_in, rl), (ch_in, ch), (cl_in, cl)]
-        )
-    ]
-
     def load(c, sem):
         source = density.at[:, :, pl.ds(pl.multiple_of(c * BS, BS), BS)]
         return pltpu.make_async_copy(source, padded.at[c + 1, pl.ds(1, bands_of_rows)], load_sem.at[sem])
 
     edges = [load(0, 0), load(mask_cols - 1, 1)]
-    small[0].start()
-    for copy in edges + small[1:]:
+    rows = [
+        pltpu.make_async_copy(density.at[at], rows_out.at[side], load_sem.at[3 + side])
+        for side, at in enumerate((0, bands_of_rows - 1))
+    ]
+    for copy in edges + rows:
         copy.start()
 
     @pl.loop(1, mask_cols - 1)
@@ -246,8 +248,12 @@
             strip = jnp.where(spot == p, pltpu.roll(edge, (p * RADIUS + side * RADIUS) % BS, 1), strip)
         strip_out[side] = strip
 
-    small[0].wait()
-    order[...] = send_order(wanted[...], me, per, mask_rows, mask_cols, col_count, capacity)
+    order[0 : wanted.shape[0]] = send_order(wanted, me, per, mask_rows, mask_cols, col_count, capacity)
+    order[wanted.shape[0] :] = known[wanted.shape[0] :]
+    to_scalars = pltpu.make_async_copy(order, table, load_sem.at[5])
+    to_scalars.start()
+    for copy in rows:
+        copy.wait()
     pl.semaphore_wait(barrier, devices - 1)
     for dr, dc in SIDES:
 
@@ -255,10 +261,10 @@
         def _():
             side_copy(dr, dc).start()
 
-    to_scalars = pltpu.make_async_copy(order, table, small_sem.at[5])
-    to_scalars.start()
+    rh[...], rl[...] = row_bands()
+    ch[...], cl[...] = col_bands()
     slots[...] = landing(
-        wanted[pl.ds(me * per, per), :], devices, mask_rows, mask_cols, col_count, capacity
+        known[pl.ds(me * per, per), :], devices, mask_rows, mask_cols, col_count, capacity
     )
     for dr, dc in SIDES:
 
@@ -281,14 +287,9 @@
 
     middle = padded.at[pl.ds(2, mask_cols - 2), pl.ds(1, bands_of_rows)]
     pltpu.make_async_copy(middle, middle, load_sem.at[2]).wait()
-    for copy in small[1:]:
-        copy.wait()
     to_scalars.wait()
 
-    @pl.loop(0, devices * capacity)
-    def _(n):
-        turn, k = n // capacity, n % capacity
-        device = target(turn)
+    def block(device, k):
         local = table[device * per, k]
         for j in range(1, per):
             local = local + table[device * per + j, k]
@@ -297,14 +298,32 @@
         before, own, after = (
             jnp.concatenate([padded[c + i, r * deep + j] for j in range(deep + 2)], axis=0) for i in range(3)
         )
-        cells = project_block(before, own, after, mask[r, c], rh, rl, ch, cl)
-        total[...] += cells
+        cells = project_block(before, own, after, table[wanted.shape[0] + r, c], rh, rl, ch, cl)
         outgoing[device, k] = cells.astype(jnp.bfloat16)
-
-        @pl.when((n % group == 0) & (n > 0) & (n <= (devices - 1) * capacity))
-        def _():
-            send(target((n - 1) // capacity), (n - 1) % capacity // group * group).start()
-
+        return cells
+
+    def turns(turn, before):
+        device = target(turn)
+
+        @pl.loop(0, capacity // group)
+        def _(p):
+            total[...] += sum(block(device, p * group + k) for k in range(group))
+
+            @pl.when(p > 0)
+            def _():
+                @pl.when(turn < devices - 1)
+                def _():
+                    send(device, (p - 1) * group).start()
+
+            @pl.when(p == 0)
+            def _():
+                @pl.when(turn > 0)
+                def _():
+                    send(before, capacity - group).start()
+
+        return device
+
+    lax.fori_loop(0, devices, turns, me)
     sums[me] = jnp.sum(total[...].reshape(BS // 8, 8, BS), axis=0)
     arrived[me] = outgoing[me]
 
@@ -333,36 +352,36 @@
     height, width = density.shape
     in_hbm = pl.BlockSpec(memory_space=pltpu.HBM)
     whole = pl.BlockSpec(memory_space=pltpu.VMEM)
-    scalar = pl.BlockSpec(memory_space=pltpu.SMEM)
     cells = devices * capacity * BS * BS
-    band = bands()
-    wanted = rebalance.reshape(-1, BS)
-    table = pltpu.VMEM(wanted.shape, jnp.int32)
+    known = jnp.concatenate([rebalance.reshape(-1, BS), jnp.pad(mask, ((0, 0), (0, BS - mask.shape[1])))])
     strips = pltpu.VMEM((2, height // STRIP, BS), jnp.float32)
+    rows = pltpu.VMEM((2, RADIUS, width), jnp.float32)
+    row_band = pltpu.VMEM((BS, BS + 2 * RADIUS), jnp.bfloat16)
+    col_band = pltpu.VMEM((2 * BS, BS), jnp.bfloat16)
     return pl.pallas_call(
-        functools.partial(exchange_kernel, sizes),
+        functools.partial(exchange_kernel, sizes, *mask.shape),
         out_shape=(
             jax.ShapeDtypeStruct((devices, capacity, BS, BS), jnp.bfloat16),
             jax.ShapeDtypeStruct((8, BS), jnp.float32),
             jax.ShapeDtypeStruct((devices, BS), jnp.int32),
         ),
-        in_specs=[scalar] + [in_hbm] * 6,
+        in_specs=[in_hbm, whole],
         out_specs=(whole, whole, whole),
         scratch_shapes=[
             pltpu.VMEM((width // BS + 2, height // RADIUS + 2, RADIUS, BS), jnp.float32),
             pltpu.VMEM((devices, capacity, BS, BS), jnp.bfloat16),
             pltpu.VMEM((BS, BS), jnp.float32),
             pltpu.VMEM((devices, 8, BS), jnp.float32),
-            table,
-            table,
-            pltpu.SMEM(wanted.shape, jnp.int32),
-        ]
-        + [pltpu.VMEM(x.shape, x.dtype) for x in band]
-        + [
+            pltpu.VMEM(known.shape, jnp.int32),
+            pltpu.SMEM(known.shape, jnp.int32),
+            row_band,
+            row_band,
+            col_band,
+            col_band,
             strips,
             strips,
-            pltpu.VMEM((2, RADIUS, width), jnp.float32),
-            pltpu.SemaphoreType.DMA((3,)),
+            rows,
+            rows,
             pltpu.SemaphoreType.DMA((6,)),
             pltpu.SemaphoreType.DMA((len(SIDES),)),
             pltpu.SemaphoreType.DMA((len(SIDES),)),
@@ -371,7 +390,7 @@
         compiler_params=pltpu.CompilerParams(vmem_limit_bytes=40 * MIB, collective_id=0, has_side_effects=True),
         cost_estimate=pl.CostEstimate(flops=cells * 2000, bytes_accessed=density.size * 4, transcendentals=cells),
         name="exchange",
-    )(mask, density.reshape(height // RADIUS, RADIUS, width), wanted, *band)
+    )(density.reshape(height // RADIUS, RADIUS, width), known)
 
 
 def place_kernel(cells, slots, arrived, volume, out, constraint, store_sem):

time: 224 us -> 214 us (0.955)
  local copies, waits for them, and re-layouts: 4.79 us -> 0 us
  Pallas kernels: 217 us -> 213 us
    unnamed x12 -> x0, local copies, waits for them, and re-layouts: 4.79 us -> none
    pallas_call x1, Pallas kernels: 212 us -> 208 us  [exchange(): pl.pallas_call(functools.partial(exchange_kernel, sizes, *mask.shape), ou...]
where the time goes in v1:
time: 214 us
  Pallas kernels  213 us (100%)
    pallas_call x1, Pallas kernels, exchange(): pl.pallas_call(functools.partial(exchange_kernel, sizes, *mask.shape), ou...  208 us
    pallas_call x1, Pallas kernels, place(): pl.pallas_call(functools.partial(place_kernel, cells), out_shape=(jax.Sha...  4.49 us

profile of v1, /device:TPU:0, one launch (start us, length us, event | category | flops | bytes accessed | tf_op | source)
XLA Modules:
  0.0 214.2 jit_solution(13359046296654580131)
XLA Ops:
  0.6 0.8 pad_add_fusion.known
  1.4 208.3 %exchange.1 = (bf16[32,8,128,128]{3,2,1,0:T(8,128)(2,1)S(1)}, f32[8,128]{1,0:T(8,128)S(1)}, s32[32,128]{1,0:T(8,128)S(1)}) custom-call(f32[64,16,4096]{2,1,0:T(8,128)} %bitcast.4, s32[72,128]{1,0:T(8,128)S(1)} %pad_add_fusion.known), custom_call_target="tpu_custom_call" | custom-call | flops 8388608000 | bytes 16777216 | tf_op jit(solution)/shard_map/exchange/pallas_call | solution.py:361
  209.7 4.5 %place.1 = (bf16[256,128,128]{2,1,0:T(8,128)(2,1)}, f32[1,1]{1,0:T(1,128)}) custom-call(s32[32,128]{1,0:T(8,128)S(1)} %get-tuple-element.7.slots, bf16[32,8,128,128]{3,2,1,0:T(8,128)(2,1)S(1)} %get-tuple-element.8.arrived, f32[8,128]{1,0:T(8,128)S(1)} %get-tuple-element.9.volume), custom_call_target="tpu_custom_call" | custom-call | bytes 16777216 | tf_op jit(solution)/shard_map/place/pallas_call | solution.py:413

commit v2 on v1

--- a/solution.py
+++ b/solution.py
@@ -16,6 +16,7 @@
 MESH = pl.DeviceIdType.MESH
 MIB = 2**20
 GROUP = 2
+SLACK = 2
 STRIP = BS // RADIUS
 SIDES = [(dr, dc) for dr in (-1, 0, 1) for dc in (-1, 0, 1) if dr or dc]
 
@@ -87,52 +88,62 @@
 
 
 def pick(chosen, rank, values, capacity):
-    lane = lax.broadcasted_iota(jnp.int32, chosen.shape, 1)
-    out = jnp.zeros(chosen.shape, jnp.int32)
-    for k in range(capacity):
-        found = jnp.sum(jnp.where(chosen & (rank == k + 1), values, 0), axis=1, keepdims=True)
-        out = jnp.where(lane == k, found, out)
-    return out
-
-
-def send_order(wanted, me, per, mask_rows, mask_cols, col_count, capacity):
-    source, local = locate(wanted, mask_rows, mask_cols, col_count)
-    mine = source == me
-    rank = upto_lane(mine.astype(jnp.int32))
-    count = jnp.broadcast_to(rank[:, BS - 1 :], rank.shape)
-    _, part = over(lax.broadcasted_iota(jnp.int32, rank.shape, 0), per)
-    for j in range(1, per):
-        rank = rank + jnp.where(part >= j, pltpu.roll(count, j, 0), 0)
-    return pick(mine, rank, local, capacity)
-
-
-def landing(wanted, devices, mask_rows, mask_cols, col_count, capacity):
-    row = lax.broadcasted_iota(jnp.int32, (devices, BS), 0)
-    lane = lax.broadcasted_iota(jnp.int32, (devices, BS), 1)
-    before = jnp.zeros((devices, 1), jnp.int32)
-    out = jnp.zeros((devices, BS), jnp.int32)
-    for j in range(wanted.shape[0]):
-        source, _ = locate(jnp.broadcast_to(wanted[j : j + 1], (devices, BS)), mask_rows, mask_cols, col_count)
-        here = source == row
-        rank = upto_lane(here.astype(jnp.int32)) + before
+    return [
+        jnp.sum(jnp.where(chosen & (rank == k + 1), values, 0), axis=1, keepdims=True) for k in range(capacity)
+    ]
+
+
+def matches(rows, capacity):
+    before, total = 0, None
+    for chosen, values in rows:
+        rank = upto_lane(chosen.astype(jnp.int32)) + before
         before = rank[:, BS - 1 :]
-        out = out + pick(here, rank, lane + j * BS, capacity)
-    return out
+        found = [pick(chosen, rank, value, capacity) for value in values]
+        total = found if total is None else [[a + b for a, b in zip(x, y)] for x, y in zip(total, found)]
+    return total
+
+
+def active_first(local, masks):
+    lane = lax.broadcasted_iota(jnp.int32, masks[0].shape, 1)
+    active = []
+    for column in local:
+        parts = [jnp.where(lane + j * BS == column, mask, 0) for j, mask in enumerate(masks)]
+        active.append(sum(jnp.sum(part, axis=1, keepdims=True) for part in parts))
+    count = sum(active)
+    ahead, behind, places = jnp.zeros_like(count), count, []
+    for one in active:
+        places.append(jnp.where(one > 0, ahead, behind))
+        ahead, behind = ahead + one, behind + 1 - one
+    return places, count
+
+
+def spread(places, columns, lane):
+    return sum(jnp.where(lane == at, column, 0) for at, column in zip(places, columns))
+
+
+def upto_row(x):
+    row = lax.broadcasted_iota(jnp.int32, x.shape, 0)
+    step = 1
+    while step < x.shape[0]:
+        x = x + jnp.where(row >= step, pltpu.roll(x, step, 0), 0)
+        step *= 2
+    return x
 
 
 def exchange_kernel(
-    sizes, mask_rows, mask_cols, density, known,
-    arrived, volume, slots, padded, outgoing, total, sums, order, table, rh, rl, ch, cl,
-    strip_out, strip_in, rows_out, rows_in, load_sem, side_send, side_recv, send_sem, recv_sem, sum_send, sum_recv,
+    sizes, mask_rows, mask_cols, spare, density, known,
+    arrived, volume, slots, most, padded, outgoing, total, sums, order, table, rh, rl, ch, cl,
+    strip_out, strip_in, rows_out, rows_in, tile, tiles, spare_out, spare_in, relay_out, plan_in, plan, load_sem,
+    side_send, side_recv, send_sem, recv_sem, sum_send, sum_recv, tile_send, tile_recv, relay_send, relay_recv, hand_sem,
 ):
     row_count, col_count = sizes
     devices, capacity = outgoing.shape[:2]
+    direct = capacity - relay_out.shape[1] if spare else capacity
     group = min(GROUP, capacity)
-    wanted = known[: known.shape[0] - mask_rows]
     bands_of_rows, _, width = density.shape
     height = bands_of_rows * RADIUS
     last = bands_of_rows + 1
-    per = wanted.shape[0] // devices
+    per = (known.shape[0] - 8) // devices
     row, col = lax.axis_index("row"), lax.axis_index("col")
     me = row * col_count + col
     half, quarter = col_count // 2, col_count // 4
@@ -141,29 +152,77 @@
     def place_of(device):
         return (device // col_count, device % col_count)
 
-    def target(turn):
-        early = 1 - turn // (3 * near)
-        is_beside = early * (turn % 3 // 2)
-        is_across = early - is_beside
-        across, beside, close = turn // 3 * 2 + turn % 3, turn // 3, (turn + 1) % near
-        far_col = ((col // half + 1) % 2) * half + (col + across) % half
-        beside_col = col // half * half + ((col // quarter + 1) % 2) * quarter + (col + beside) % quarter
-        close_col = col // quarter * quarter + (col + close) % quarter
-        to_col = is_across * far_col + is_beside * beside_col + (1 - early) * close_col
-        step = is_across * (across // half) + is_beside * (beside // quarter) + (1 - early) * (close // quarter)
-        return (row + step) % row_count * col_count + to_col
-
-    def send(device, k):
-        part = pl.ds(k, group)
+    def flip(x, by):
+        out, bit = 0, 1
+        while bit < max(row_count, col_count):
+            out = out + (x // bit + by // bit) % 2 * bit
+            bit *= 2
+        return out
+
+    def far(i):
+        return flip(row, i // half) * col_count + flip(col, half + i % half)
+
+    def beside(i):
+        return flip(row, i // quarter) * col_count + flip(col, quarter + i % quarter)
+
+    def close(i):
+        return flip(row, i // quarter) * col_count + flip(col, i % quarter)
+
+    def mate(i):
+        late = i // near
+        return (1 - late) * beside(i % near) + late * close((i + 1) % near)
+
+    partner = far(0)
+    side = col // quarter
+    outer = (side // 3) + (3 - side) // 3
+
+    def task(t):
+        second, late = t // near % 2, t // (2 * near)
+        i = t % near
+        is_far = (1 - late) * (outer * second + (1 - outer)) + late * outer * (1 - second)
+        is_beside = outer * (1 - late) * (1 - second) + (1 - outer) * late * (1 - second)
+        far_at = i + near * (outer * late + (1 - outer) * second)
+        device = is_far * far(far_at) + is_beside * beside(i) + (1 - is_far - is_beside) * close((i + 1) % near)
+        return device, is_far * direct + (1 - is_far) * capacity
+
+    def send(device, k, n=0):
+        part = pl.ds(k, n or group)
         return pltpu.make_async_remote_copy(
             src_ref=outgoing.at[device, part], dst_ref=arrived.at[me, part], send_sem=send_sem.at[device],
             recv_sem=recv_sem.at[me], device_id=place_of(device), device_id_type=MESH,
         )
 
-    def receive(device):
-        return pltpu.make_async_remote_copy(
-            src_ref=outgoing.at[device], dst_ref=arrived.at[device], send_sem=send_sem.at[device],
+    def receive(device, count):
+        part = pl.ds(0, count)
+        return pltpu.make_async_remote_copy(
+            src_ref=outgoing.at[device, part], dst_ref=arrived.at[device, part], send_sem=send_sem.at[device],
             recv_sem=recv_sem.at[device], device_id=place_of(device), device_id_type=MESH,
+        )
+
+    def tile_copy(device, source):
+        return pltpu.make_async_remote_copy(
+            src_ref=tile, dst_ref=tiles.at[source], send_sem=tile_send.at[device],
+            recv_sem=tile_recv.at[source], device_id=place_of(device), device_id_type=MESH,
+        )
+
+    def spare_copy(p, count):
+        part = pl.ds(p, count)
+        return pltpu.make_async_remote_copy(
+            src_ref=spare_out.at[part], dst_ref=spare_in.at[part], send_sem=hand_sem.at[0],
+            recv_sem=hand_sem.at[1], device_id=place_of(partner), device_id_type=MESH,
+        )
+
+    def plan_copy():
+        return pltpu.make_async_remote_copy(
+            src_ref=order.at[pl.ds(0, devices)], dst_ref=plan_in, send_sem=hand_sem.at[2],
+            recv_sem=hand_sem.at[3], device_id=place_of(partner), device_id_type=MESH,
+        )
+
+    def relay_copy(i, device, source):
+        return pltpu.make_async_remote_copy(
+            src_ref=relay_out.at[i], dst_ref=arrived.at[source, pl.ds(direct, capacity - direct)],
+            send_sem=relay_send.at[device], recv_sem=relay_recv.at[source], device_id=place_of(device),
+            device_id_type=MESH,
         )
 
     def send_sum(device):
@@ -248,10 +307,6 @@
             strip = jnp.where(spot == p, pltpu.roll(edge, (p * RADIUS + side * RADIUS) % BS, 1), strip)
         strip_out[side] = strip
 
-    order[0 : wanted.shape[0]] = send_order(wanted, me, per, mask_rows, mask_cols, col_count, capacity)
-    order[wanted.shape[0] :] = known[wanted.shape[0] :]
-    to_scalars = pltpu.make_async_copy(order, table, load_sem.at[5])
-    to_scalars.start()
     for copy in rows:
         copy.wait()
     pl.semaphore_wait(barrier, devices - 1)
@@ -261,11 +316,43 @@
         def _():
             side_copy(dr, dc).start()
 
+    shape = (devices, BS)
+    device_of, lane = (lax.broadcasted_iota(jnp.int32, shape, d) for d in range(2))
+    rows_of = []
+    for j in range(per):
+        source, local = locate(known[pl.ds(j, devices, stride=per)], mask_rows, mask_cols, col_count)
+        rows_of.append((source == me, [local]))
+    (local,) = matches(rows_of, capacity)
+    masks = [jnp.broadcast_to(known[devices * per + j : devices * per + j + 1], shape) for j in range(per)]
+    places, count = active_first(local, masks)
+    sorted_local = spread(places, local, lane)
+    in_rank = (lane >= capacity) & (lane < 2 * capacity) & (lane - capacity < count)
+    order[0:devices] = sorted_local + jnp.where(in_rank, 1, 0)
+    order[devices:] = jnp.zeros((8, BS), jnp.int32)
+    tile[...] = known[devices * per : devices * per + per]
+    if spare:
+        _, at_col = over(device_of, col_count)
+        away = over(at_col, half)[0] != col // half
+        extra = [(away & (count > k)).astype(jnp.int32) for k in range(direct, capacity)]
+        upto = upto_row(sum(extra))
+        at = upto - sum(extra)
+        lists, hand = jnp.zeros((1, BS), jnp.int32), jnp.zeros(shape, jnp.int32)
+        for k, one in zip(range(direct, capacity), extra):
+            picked = jnp.sum(jnp.where(lane == k, sorted_local, 0), axis=1, keepdims=True)
+            lists = lists + jnp.sum(jnp.where((one > 0) & (at == lane), picked, 0), axis=0, keepdims=True)
+            held = jnp.where((one > 0) & (at < spare), at, spare)
+            hand = hand + jnp.where(lane == 2 * capacity + k, held, 0)
+            at = at + one
+        full = upto[devices - 1 :]
+        order[0:devices] = order[0:devices] + hand
+        order[devices : devices + 1] = lists
+        order[devices + 1 : devices + 2] = (lane[0:1] < full).astype(jnp.int32)
+        tile[...] = tile[...] + 2 * full
+        spare_in[spare] = jnp.zeros((BS, BS), jnp.bfloat16)
+    to_scalars = pltpu.make_async_copy(order, table, load_sem.at[5])
+    to_scalars.start()
     rh[...], rl[...] = row_bands()
     ch[...], cl[...] = col_bands()
-    slots[...] = landing(
-        known[pl.ds(me * per, per), :], devices, mask_rows, mask_cols, col_count, capacity
-    )
     for dr, dc in SIDES:
 
         @pl.when(there(-dr, -dc))
@@ -289,47 +376,138 @@
     pltpu.make_async_copy(middle, middle, load_sem.at[2]).wait()
     to_scalars.wait()
 
-    def block(device, k):
-        local = table[device * per, k]
-        for j in range(1, per):
-            local = local + table[device * per + j, k]
+
+    @pl.loop(1, devices)
+    def _(o):
+        tile_copy((me + o) % devices, me).start()
+
+    tiles[me] = tile[...]
+    if spare:
+        plan_copy().start()
+
+    def block(local, active):
         r, c = over(local, mask_cols)
         deep = BS // RADIUS
         before, own, after = (
             jnp.concatenate([padded[c + i, r * deep + j] for j in range(deep + 2)], axis=0) for i in range(3)
         )
-        cells = project_block(before, own, after, table[wanted.shape[0] + r, c], rh, rl, ch, cl)
-        outgoing[device, k] = cells.astype(jnp.bfloat16)
-        return cells
-
-    def turns(turn, before):
-        device = target(turn)
-
-        @pl.loop(0, capacity // group)
+        return project_block(before, own, after, active, rh, rl, ch, cl)
+
+    def turn(device, blocks, pending, opening):
+        @pl.loop(0, lax.div(blocks, group))
         def _(p):
-            total[...] += sum(block(device, p * group + k) for k in range(group))
+            cells = []
+            for k in range(group):
+                active = table[device, capacity + p * group + k]
+                cells.append(block(table[device, p * group + k], active))
+                outgoing[device, p * group + k] = cells[k].astype(jnp.bfloat16)
+            total[...] += sum(cells)
+            pl.when(p == 0)(pending)
+
+            @pl.when((p > 0) & opening)
+            def _():
+                send(device, (p - 1) * group).start()
+
+    def follow(before):
+        device, blocks = before
+        if direct == capacity:
+            send(device, 0, capacity).start()
+            return
+        pl.when(blocks == direct)(lambda: send(device, 0, direct).start())
+        pl.when(blocks == capacity)(lambda: send(device, 0, capacity).start())
+
+    def steps(start, stop, first, before):
+        def step(t, before):
+            device, blocks = task(t)
+
+            def pending():
+                pl.when(t == start)(first)
+                if start == 0:
+                    pl.when(t == 1)(lambda: send(before[0], before[1] - group).start())
+                pl.when(t > max(start, 1))(lambda: follow(before))
+
+            turn(device, blocks, pending, t == 0)
+            return device, blocks
+
+        return lax.fori_loop(start, stop, step, before)
+
+    def relay():
+        plan_copy().wait()
+        to_plan = pltpu.make_async_copy(plan_in, plan, load_sem.at[0])
+        to_plan.start()
+        to_plan.wait()
+        spare_copy(0, spare).wait()
+
+        @pl.loop(0, 2 * near)
+        def _(i):
+            for k in range(direct, capacity):
+                relay_out[i, k - direct] = spare_in[plan[mate(i), 2 * capacity + k]]
+
+            @pl.when(i > 0)
+            def _():
+                relay_copy(i - 1, mate(i - 1), partner).start()
+
+        arrived[partner, direct:] = relay_out[2 * near - 1]
+
+    before = steps(0, near, lambda: None, (me, capacity))
+    if spare:
+
+        @pl.loop(0, spare // group)
+        def _(p):
+            cells = []
+            for k in range(group):
+                cells.append(block(table[devices, p * group + k], table[devices + 1, p * group + k]))
+                spare_out[p * group + k] = cells[k].astype(jnp.bfloat16)
+            total[...] += sum(cells)
+            pl.when(p == 0)(lambda: follow(before))
 
             @pl.when(p > 0)
             def _():
-                @pl.when(turn < devices - 1)
-                def _():
-                    send(device, (p - 1) * group).start()
-
-            @pl.when(p == 0)
-            def _():
-                @pl.when(turn > 0)
-                def _():
-                    send(before, capacity - group).start()
-
-        return device
-
-    lax.fori_loop(0, devices, turns, me)
-    sums[me] = jnp.sum(total[...].reshape(BS // 8, 8, BS), axis=0)
+                spare_copy((p - 1) * group, group).start()
+
+        before = steps(near, 2 * near, lambda: spare_copy(spare - group, group).start(), before)
+        pl.when(outer == 1)(relay)
+        steps(2 * near, 4 * near, lambda: follow(before), before)
+        pl.when(outer == 0)(relay)
+    else:
+        steps(near, 4 * near, lambda: follow(before), before)
+
+    sums[me] = jnp.sum(total[...], axis=0, keepdims=True)
     arrived[me] = outgoing[me]
 
     @pl.loop(1, devices)
     def _(o):
         send_sum((me + o) % devices).start()
+
+    @pl.loop(1, devices)
+    def _(o):
+        other = (me + o) % devices
+        tile_copy(other, other).wait()
+
+    rows_in_order = []
+    for j in range(per):
+        mine = jnp.broadcast_to(known[pl.ds(me * per + j, 1)], shape)
+        source, local = locate(mine, mask_rows, mask_cols, col_count)
+        rows_in_order.append((source == device_of, [local, lane + j * BS]))
+    local, slot = matches(rows_in_order, capacity)
+    places, _ = active_first(local, [tiles[:, j] & 1 for j in range(per)])
+    slots[...] = spread(places, slot, lane)
+    most[...] = jnp.max(tiles[:, 0] >> 1, axis=0, keepdims=True)
+
+    @pl.loop(0, 2 * near)
+    def _(i):
+        receive(far(i), direct).wait()
+
+    @pl.loop(0, 2 * near - 1)
+    def _(i):
+        receive(mate(i), capacity).wait()
+
+    if spare:
+
+        @pl.loop(0, 2 * near - 1)
+        def _(i):
+            relay_copy(i, mate(i), partner).wait_send()
+            relay_copy(i, mate(i), far(i + 1)).wait_recv()
 
     @pl.loop(1, devices)
     def _(o):
@@ -339,41 +517,41 @@
 
     volume[...] = jnp.sum(sums[...], axis=0)
 
-    @pl.loop(1, devices)
-    def _(o):
-        other = (me + o) % devices
-        receive(other).wait_send()
-        receive(other).wait_recv()
-
-
-def exchange(mask, density, rebalance, sizes):
+
+def exchange(mask_shape, density, known, sizes, lean):
     devices = sizes[0] * sizes[1]
-    capacity = mask.size // devices
+    capacity = mask_shape[0] * mask_shape[1] // devices
+    extra = capacity // 4
+    lean = lean and extra > 0
+    spare = (devices // 2 + SLACK) // GROUP * GROUP if lean else 0
     height, width = density.shape
     in_hbm = pl.BlockSpec(memory_space=pltpu.HBM)
     whole = pl.BlockSpec(memory_space=pltpu.VMEM)
     cells = devices * capacity * BS * BS
-    known = jnp.concatenate([rebalance.reshape(-1, BS), jnp.pad(mask, ((0, 0), (0, BS - mask.shape[1])))])
     strips = pltpu.VMEM((2, height // STRIP, BS), jnp.float32)
     rows = pltpu.VMEM((2, RADIUS, width), jnp.float32)
     row_band = pltpu.VMEM((BS, BS + 2 * RADIUS), jnp.bfloat16)
     col_band = pltpu.VMEM((2 * BS, BS), jnp.bfloat16)
+    plan = (devices, BS)
+    per = devices * capacity // BS
+    blocks = lambda *n: pltpu.VMEM((*n, BS, BS), jnp.bfloat16)
     return pl.pallas_call(
-        functools.partial(exchange_kernel, sizes, *mask.shape),
+        functools.partial(exchange_kernel, sizes, *mask_shape, spare),
         out_shape=(
             jax.ShapeDtypeStruct((devices, capacity, BS, BS), jnp.bfloat16),
-            jax.ShapeDtypeStruct((8, BS), jnp.float32),
-            jax.ShapeDtypeStruct((devices, BS), jnp.int32),
+            jax.ShapeDtypeStruct((1, BS), jnp.float32),
+            jax.ShapeDtypeStruct(plan, jnp.int32),
+            jax.ShapeDtypeStruct((1, BS), jnp.int32),
         ),
         in_specs=[in_hbm, whole],
-        out_specs=(whole, whole, whole),
+        out_specs=(whole, whole, whole, whole),
         scratch_shapes=[
             pltpu.VMEM((width // BS + 2, height // RADIUS + 2, RADIUS, BS), jnp.float32),
-            pltpu.VMEM((devices, capacity, BS, BS), jnp.bfloat16),
+            blocks(devices, capacity),
             pltpu.VMEM((BS, BS), jnp.float32),
-            pltpu.VMEM((devices, 8, BS), jnp.float32),
-            pltpu.VMEM(known.shape, jnp.int32),
-            pltpu.SMEM(known.shape, jnp.int32),
+            pltpu.VMEM((devices, 1, BS), jnp.float32),
+            pltpu.VMEM((devices + 8, BS), jnp.int32),
+            pltpu.SMEM((devices + 8, BS), jnp.int32),
             row_band,
             row_band,
             col_band,
@@ -382,15 +560,25 @@
             strips,
             rows,
             rows,
+            pltpu.VMEM((per, BS), jnp.int32),
+            pltpu.VMEM((devices, per, BS), jnp.int32),
+            blocks(max(spare, 1)),
+            blocks(spare + 1),
+            blocks(devices // 2 if lean else 1, max(extra, 1)),
+            pltpu.VMEM(plan, jnp.int32),
+            pltpu.SMEM(plan, jnp.int32),
             pltpu.SemaphoreType.DMA((6,)),
             pltpu.SemaphoreType.DMA((len(SIDES),)),
             pltpu.SemaphoreType.DMA((len(SIDES),)),
         ]
-        + [pltpu.SemaphoreType.DMA((devices,))] * 4,
-        compiler_params=pltpu.CompilerParams(vmem_limit_bytes=40 * MIB, collective_id=0, has_side_effects=True),
+        + [pltpu.SemaphoreType.DMA((devices,))] * 8
+        + [pltpu.SemaphoreType.DMA((4,))],
+        compiler_params=pltpu.CompilerParams(
+            vmem_limit_bytes=44 * MIB, collective_id=0 if lean else 1, has_side_effects=True
+        ),
         cost_estimate=pl.CostEstimate(flops=cells * 2000, bytes_accessed=density.size * 4, transcendentals=cells),
-        name="exchange",
-    )(density.reshape(height // RADIUS, RADIUS, width), known)
+        name="exchange_lean" if lean else "exchange",
+    )(density.reshape(height // RADIUS, RADIUS, width), known), spare
 
 
 def place_kernel(cells, slots, arrived, volume, out, constraint, store_sem):
@@ -427,8 +615,20 @@
 
 def per_device(density, design_mask, rebalance):
     sizes = (lax.axis_size("row"), lax.axis_size("col"))
-    arrived, volume, slots = exchange(design_mask, density, rebalance, sizes)
-    balanced, constraint = place(slots, arrived, volume, float(density.size * sizes[0] * sizes[1]))
+    shape = design_mask.shape
+    cells = float(density.size * sizes[0] * sizes[1])
+    flat = design_mask.reshape(-1, BS)
+    known = jnp.concatenate([rebalance.reshape(-1, BS), jnp.pad(flat, ((0, 8 - flat.shape[0]), (0, 0)))])
+
+    def full():
+        (arrived, volume, slots, _), _ = exchange(shape, density, known, sizes, False)
+        return place(slots, arrived, volume, cells)
+
+    if design_mask.size // (sizes[0] * sizes[1]) < 4:
+        balanced, constraint = full()
+        return balanced, constraint[0, 0]
+    (arrived, volume, slots, most), spare = exchange(shape, density, known, sizes, True)
+    balanced, constraint = lax.cond(most[0, 0] > spare, full, lambda: place(slots, arrived, volume, cells))
     return balanced, constraint[0, 0]
 
 

time: 214 us -> 199 us (0.930)
  Pallas kernels: 213 us -> 196 us
    pallas_call x1, Pallas kernels: 208 us -> 192 us  [exchange(): pl.pallas_call(functools.partial(exchange_kernel, sizes, *mask_shape, spa...]
where the time goes in v2:
time: 199 us; the launch traced here: 198 us
  Pallas kernels  196 us (98%)
    pallas_call x1, Pallas kernels, exchange(): pl.pallas_call(functools.partial(exchange_kernel, sizes, *mask_shape, spa...  192 us
    pallas_call x1, Pallas kernels, place(): pl.pallas_call(functools.partial(place_kernel, cells), out_shape=(jax.Sha...  4.49 us

profile of v2, /device:TPU:0, one launch (start us, length us, event | category | flops | bytes accessed | tf_op | source)
XLA Modules:
  0.0 198.3 jit_solution(11122794668161894490)
XLA Ops:
  0.6 0.8 reshape.22
  1.4 0.8 pad_add_fusion.known
  2.2 191.6 %exchange_lean.1 = (bf16[32,8,128,128]{3,2,1,0:T(8,128)(2,1)S(1)}, f32[1,128]{1,0:T(1,128)S(1)}, s32[32,128]{1,0:T(8,128)S(1)}, s32[1,128]{1,0:T(1,128)S(1)}) custom-call(f32[64,16,4096]{2,1,0:T(8,128)} %bitcast.9, s32[72,128]{1,0:T(8,128)S(1)} %pad_add_fusion.known), custom_call_target="tpu_custom_call" | custom-call | flops 8388608000 | bytes 16777216 | tf_op jit(solution)/shard_map/exchange_lean/pallas_call | solution.py:538
  193.8 4.5 %conditional.1 = (bf16[256,128,128]{2,1,0:T(8,128)(2,1)}, f32[]{:T(128)}) conditional(s32[]{:T(128)} %bitcast.5, (s32[32,128]{1,0:T(8,128)S(1)}, bf16[32,8,128,128]{3,2,1,0:T(8,128)(2,1)S(1)}, f32[1,128]{1,0:T(1,128)S(1)}) %tuple.17, (f32[1024,4096]{1,0:T(8,128)}, s32[72,128]{1,0:T(8,128)S(1)}) %tuple.18), branch_computations={%region_0.1_spmd, %region_1.2_spmd} | conditional | flops 8388608000 | bytes 33554448 | solution.py:631
  193.8 4.5 %place.2 = (bf16[256,128,128]{2,1,0:T(8,128)(2,1)}, f32[1,1]{1,0:T(1,128)}) custom-call(s32[32,128]{1,0:T(8,128)S(1)} %get-tuple-element.15.slots, bf16[32,8,128,128]{3,2,1,0:T(8,128)(2,1)S(1)} %get-tuple-element.16.arrived, f32[1,128]{1,0:T(1,128)S(1)} %get-tuple-element.17.volume), custom_call_target="tpu_custom_call" | custom-call | bytes 16777216 | tf_op jit(solution)/shard_map/cond/branch_0_fun/place/pallas_call | solution.py:601

commit v3 on v2

--- a/solution.py
+++ b/solution.py
@@ -179,9 +179,10 @@
     def task(t):
         second, late = t // near % 2, t // (2 * near)
         i = t % near
-        is_far = (1 - late) * (outer * second + (1 - outer)) + late * outer * (1 - second)
-        is_beside = outer * (1 - late) * (1 - second) + (1 - outer) * late * (1 - second)
-        far_at = i + near * (outer * late + (1 - outer) * second)
+        same = outer * second + (1 - outer) * (1 - second)
+        is_far = (1 - late) * same + late * (1 - second)
+        is_beside = (1 - late) * (1 - same)
+        far_at = i + near * late
         device = is_far * far(far_at) + is_beside * beside(i) + (1 - is_far - is_beside) * close((i + 1) % near)
         return device, is_far * direct + (1 - is_far) * capacity
 

time: 199 us -> 194 us (0.975)
  Pallas kernels: 196 us -> 191 us
    pallas_call x1, Pallas kernels: 192 us -> 187 us  [exchange(): pl.pallas_call(functools.partial(exchange_kernel, sizes, *mask_shape, spa...]
where the time goes in v3:
time: 194 us; the launch traced here: 193 us
  Pallas kernels  191 us (98%)
    pallas_call x1, Pallas kernels, exchange(): pl.pallas_call(functools.partial(exchange_kernel, sizes, *mask_shape, spa...  187 us
    pallas_call x1, Pallas kernels, place(): pl.pallas_call(functools.partial(place_kernel, cells), out_shape=(jax.Sha...  4.49 us

profile of v3, /device:TPU:0, one launch (start us, length us, event | category | flops | bytes accessed | tf_op | source)
XLA Modules:
  0.0 193.3 jit_solution(14218350337009788386)
XLA Ops:
  0.6 0.8 reshape.22
  1.4 0.8 pad_add_fusion.known
  2.2 186.6 %exchange_lean.1 = (bf16[32,8,128,128]{3,2,1,0:T(8,128)(2,1)S(1)}, f32[1,128]{1,0:T(1,128)S(1)}, s32[32,128]{1,0:T(8,128)S(1)}, s32[1,128]{1,0:T(1,128)S(1)}) custom-call(f32[64,16,4096]{2,1,0:T(8,128)} %bitcast.9, s32[72,128]{1,0:T(8,128)S(1)} %pad_add_fusion.known), custom_call_target="tpu_custom_call" | custom-call | flops 8388608000 | bytes 16777216 | tf_op jit(solution)/shard_map/exchange_lean/pallas_call | solution.py:539
  188.8 4.5 %conditional.1 = (bf16[256,128,128]{2,1,0:T(8,128)(2,1)}, f32[]{:T(128)}) conditional(s32[]{:T(128)} %bitcast.5, (s32[32,128]{1,0:T(8,128)S(1)}, bf16[32,8,128,128]{3,2,1,0:T(8,128)(2,1)S(1)}, f32[1,128]{1,0:T(1,128)S(1)}) %tuple.17, (f32[1024,4096]{1,0:T(8,128)}, s32[72,128]{1,0:T(8,128)S(1)}) %tuple.18), branch_computations={%region_0.1_spmd, %region_1.2_spmd} | conditional | flops 8388608000 | bytes 33554448 | solution.py:632
  188.8 4.5 %place.2 = (bf16[256,128,128]{2,1,0:T(8,128)(2,1)}, f32[1,1]{1,0:T(1,128)}) custom-call(s32[32,128]{1,0:T(8,128)S(1)} %get-tuple-element.15.slots, bf16[32,8,128,128]{3,2,1,0:T(8,128)(2,1)S(1)} %get-tuple-element.16.arrived, f32[1,128]{1,0:T(1,128)S(1)} %get-tuple-element.17.volume), custom_call_target="tpu_custom_call" | custom-call | bytes 16777216 | tf_op jit(solution)/shard_map/cond/branch_0_fun/place/pallas_call | solution.py:602
